TPU v7x, 32 devices: a whole 2x2x4 slice. The times are simulated.
32 devices in a mesh: row: 4 (over x, core), col: 8 (over z, y).
Axes of the slice: x: 2, y: 2, z: 4, core: 2. Of those that a mesh axis runs over, the one named last changes fastest.
Arguments:
- pressure_rhs: bfloat16 [384, 256, 384], P('col', 'row'), may hold values from -10 to 10, as said below
- scalar_source: bfloat16 [384, 256, 384], P('col', 'row'), may hold values from -10 to 10, as said below
- forward_y: bfloat16 [256, 256], replicated, may hold values from -0.375 to 0.375
- back_y: bfloat16 [256, 256], replicated, may hold values from -0.375 to 0.375
- wall_rates: float32 [256], replicated, may hold values from 0.05 to 4
Outputs:
- pressure: bfloat16 [384, 256, 384], P('col', 'row')
- scalar: bfloat16 [384, 256, 384], P('col', 'row')
Inputs may be any that keep to these rules, and one draw needn't show every extreme that they name: `pressure_rhs`: a real field of order one. `scalar_source`: a real field of order one.
All inputs are finite; a program needn't handle non-finite values.
Results may differ from a plain program's by a relative error of at most 0.012.
Values may be sent and summed in bfloat16 or wider, within the bound.
A program may use at most 64 MiB of HBM per device.

v0:
```python
import math

import jax
import jax.numpy as jnp
from jax import lax
from jax.sharding import PartitionSpec as P

KEEP = 256


diffusion = 0.5


def x_table(width, groups):
    half = width // 2
    per = half // groups
    column = lax.broadcasted_iota(jnp.int32, (width, width), 1)
    place = lax.broadcasted_iota(jnp.int32, (width, width), 0)
    owner = column // (2 * per)
    part = column // per % 2
    mode = owner * per + column % per
    phase = mode * place % width
    angle = phase.astype(jnp.float32) * (2.0 * math.pi / width)
    factor = math.sqrt(2.0 / width)
    return jnp.where(part == 0, factor * jnp.cos(angle), -factor * jnp.sin(angle)).astype(
        jnp.bfloat16
    )


def x_back_table(width, groups):
    half = width // 2
    per = half // groups
    line = lax.broadcasted_iota(jnp.int32, (width, width), 0)
    place = lax.broadcasted_iota(jnp.int32, (width, width), 1)
    owner = line // (2 * per)
    part = line // per % 2
    mode = owner * per + line % per
    phase = mode * place % width
    angle = phase.astype(jnp.float32) * (2.0 * math.pi / width)
    weight = jnp.where(mode == 0, 0.5, 1.0) * math.sqrt(2.0 / width)
    return jnp.where(part == 0, weight * jnp.cos(angle), -weight * jnp.sin(angle)).astype(
        jnp.bfloat16
    )


def z_tables(wave, length):
    place = lax.iota(jnp.int32, length)
    phase = wave[:, None] * place[None, :] % length
    angle = phase.astype(jnp.float32) * (2.0 * math.pi / length)
    factor = 1.0 / math.sqrt(length)
    return (
        (factor * jnp.cos(angle)).astype(jnp.bfloat16),
        (factor * jnp.sin(angle)).astype(jnp.bfloat16),
    )


def shards(pressure_rhs, scalar_source, forward_y, back_y, wall_rates):
    rows = lax.axis_size("row")
    cols = lax.axis_size("col")
    row_at = lax.axis_index("row")
    col_at = lax.axis_index("col")
    depth_local, height_local, width = pressure_rhs.shape
    height = forward_y.shape[0]
    depth = depth_local * cols
    per = width // (2 * cols)
    wave = lax.iota(jnp.int32, KEEP)
    wave = jnp.where(wave < KEEP // 2, wave, wave + (depth - KEEP))
    count = wave.shape[0]
    count_local = count // rows
    cosz, sinz = z_tables(wave, depth)
    table_x = x_table(width, cols)
    back_x = x_back_table(width, cols)
    fields = jnp.stack((pressure_rhs, scalar_source))
    spectra = jnp.dot(fields.reshape(-1, width), table_x, preferred_element_type=jnp.float32)
    spectra = spectra.astype(jnp.bfloat16).reshape(2, depth_local, height_local, width)
    block = lax.all_to_all(spectra, "col", split_axis=3, concat_axis=1, tiled=True)
    items = block.shape[2]
    flat = block.reshape(2, depth, -1)
    first = jnp.einsum("fzq,nz->fqn", flat, cosz, preferred_element_type=jnp.float32)
    second = jnp.einsum("fzq,nz->fqn", flat, sinz, preferred_element_type=jnp.float32)
    first = first.reshape(2, items, 2, per, count)
    second = second.reshape(2, items, 2, per, count)
    real = first[:, :, 0] + second[:, :, 1]
    imag = first[:, :, 1] - second[:, :, 0]
    zmodes = jnp.stack((real, imag), axis=2).astype(jnp.bfloat16)
    lines = lax.all_to_all(zmodes, "row", split_axis=4, concat_axis=1, tiled=True)
    coeffs = jnp.einsum(
        "jy,fyq->fjq", forward_y, lines.reshape(2, height, -1), preferred_element_type=jnp.float32
    )
    coeffs = coeffs.reshape(2, height, 2, per, count_local)
    modes_x = col_at * per + lax.iota(jnp.int32, per)
    modes_z = lax.dynamic_slice_in_dim(wave, row_at * count_local, count_local)
    signed = jnp.where(modes_z < depth // 2, modes_z, modes_z - depth)
    alive = (modes_z < KEEP // 2) | (modes_z >= depth - KEEP // 2)
    kx_sq = (modes_x.astype(jnp.float32) * (2.0 * math.pi / width)) ** 2
    kz_sq = (signed.astype(jnp.float32) * (2.0 * math.pi / depth)) ** 2
    wave_sq = kx_sq[:, None] + kz_sq[None, :]
    total = wave_sq[None, :, :] + wall_rates[:, None, None]
    hat_pressure = coeffs[0] / (-total)[:, None]
    hat_scalar = coeffs[1] / (1.0 + diffusion * total)[:, None]
    hats = jnp.where(alive, jnp.stack((hat_pressure, hat_scalar)), 0.0).astype(jnp.bfloat16)
    solved = jnp.einsum(
        "yj,fjq->fyq", back_y, hats.reshape(2, height, -1), preferred_element_type=jnp.float32
    )
    solved = solved.astype(jnp.bfloat16).reshape(2, height, 2, per, count_local)
    block = lax.all_to_all(solved, "row", split_axis=1, concat_axis=4, tiled=True)
    first = jnp.einsum("fypkn,nz->fzypk", block, cosz, preferred_element_type=jnp.float32)
    second = jnp.einsum("fypkn,nz->fzypk", block, sinz, preferred_element_type=jnp.float32)
    real = first[:, :, :, 0] - second[:, :, :, 1]
    imag = first[:, :, :, 1] + second[:, :, :, 0]
    zlines = jnp.stack((real, imag), axis=3).astype(jnp.bfloat16)
    zlines = zlines.reshape(2, depth, height_local, 2 * per)
    block = lax.all_to_all(zlines, "col", split_axis=1, concat_axis=3, tiled=True)
    result = jnp.dot(block.reshape(-1, width), back_x, preferred_element_type=jnp.float32)
    result = result.astype(jnp.bfloat16).reshape(block.shape)
    return (result[0], result[1])


def solution(mesh):
    placed = (P("col", "row", None), P("col", "row", None), P(), P(), P())
    return jax.shard_map(
        shards,
        mesh=mesh,
        in_specs=placed,
        out_specs=(P("col", "row", None), P("col", "row", None)),
        check_vma=False,
    )
```

profile of v0, /device:TPU:0, one launch (start us, length us, event | category | flops | bytes accessed | tf_op | source)
XLA Modules:
  0.0 582.0 jit_solution(5232312488892164628)
XLA Ops:
  10.9 14.4 %copy.27 = bf16[2,48,64,384]{2,1,0,3:T(8,128)(2,1)} copy(bf16[2,48,64,384]{3,2,1,0:T(8,128)(2,1)} %bitcast.97) | data formatting | bytes 9437184 | tf_op jit(solution)/shard_map/reshape | solution.py:75
  25.4 11.3 %reshape.118 = bf16[8,2,147456]{2,1,0:T(2,128)(2,1)} reshape(bf16[384,2,48,64]{3,2,1,0:T(8,128)(2,1)} %bitcast.83) | data formatting | bytes 9437184
  36.7 7.5 %all-to-all-start = ((bf16[8,2,147456]{2,1,0:T(2,128)(2,1)}), bf16[8,2,147456]{2,1,0:T(2,128)(2,1)}, u32[]{:S(2)}, u32[]{:S(2)}) async-start(bf16[8,2,147456]{2,1,0:T(2,128)(2,1)} %reshape.118), calls=%async_computation | async-start | bytes 9437184 | tf_op jit(solution)/shard_map/all_to_all | solution.py:76
  44.2 104.4 %all-to-all-done = bf16[8,2,147456]{2,1,0:T(2,128)(2,1)} async-done(((bf16[8,2,147456]{2,1,0:T(2,128)(2,1)}), bf16[8,2,147456]{2,1,0:T(2,128)(2,1)}, u32[]{:S(2)}, u32[]{:S(2)}) %all-to-all-start) | async-done | bytes 4718624 | tf_op jit(solution)/shard_map/all_to_all | solution.py:76
  148.7 11.1 %reshape.119 = bf16[384,2,48,64]{3,2,1,0:T(8,128)(2,1)} reshape(bf16[8,2,147456]{2,1,0:T(2,128)(2,1)} %all-to-all-done) | data formatting | bytes 9437184
  159.8 16.2 %copy.29 = bf16[2,8,48,64,48]{4,3,2,1,0:T(8,128)(2,1)} copy(bf16[2,8,48,64,48]{3,2,0,4,1:T(8,128)(2,1)} %bitcast.86) | data formatting | bytes 9437184 | tf_op jit(solution)/shard_map/all_to_all | solution.py:76
  176.0 23.8 %reshape.110 = bf16[2,384,3072]{2,1,0:T(8,128)(2,1)} reshape(bf16[2,8,48,64,48]{4,3,2,1,0:T(8,128)(2,1)} %copy.29) | data formatting | bytes 9437184 | tf_op jit(solution)/shard_map/reshape | solution.py:78
  217.2 10.5 %copy.31 = bf16[2,64,2,24,256]{1,3,2,0,4:T(8,128)(2,1)} copy(bf16[2,64,2,24,256]{4,3,2,1,0:T(8,128)(2,1)S(1)} %pad_maximum_fusion.2) | data formatting | bytes 6291456 | tf_op jit(solution)/shard_map/stack | solution.py:85
  227.8 7.8 %reshape.120 = bf16[4,2,196608]{2,1,0:T(2,128)(2,1)} reshape(bf16[256,2,2,24,64]{4,3,2,1,0:T(8,128)(2,1)} %bitcast.87) | data formatting | bytes 6291456
  241.9 34.6 %all-to-all-done.1 = bf16[4,2,196608]{2,1,0:T(2,128)(2,1)S(1)} async-done(((bf16[4,2,196608]{2,1,0:T(2,128)(2,1)}), bf16[4,2,196608]{2,1,0:T(2,128)(2,1)S(1)}, u32[]{:S(2)}, u32[]{:S(2)}) %all-to-all-start.1) | async-done | bytes 3145760 | tf_op jit(solution)/shard_map/all_to_all | solution.py:86
  281.8 10.2 %copy.47 = bf16[2,64,2,24,4,64]{1,4,5,3,2,0:T(4,128)(2,1)} copy(bf16[2,64,2,24,4,64]{1,3,2,0,5,4:T(8,128)(2,1)} %bitcast.88) | data formatting | bytes 6291456 | tf_op jit(solution)/shard_map/all_to_all | solution.py:86
  292.0 8.7 %reshape.111 = bf16[2,256,3072]{1,2,0:T(8,128)(2,1)S(1)} reshape(bf16[2,4,64,2,24,64]{2,1,5,4,3,0:T(4,128)(2,1)} %bitcast.89) | data formatting | bytes 6291456 | tf_op jit(solution)/shard_map/reshape | solution.py:88
  306.5 9.5 %copy.33 = bf16[2,256,2,24,64]{4,3,2,0,1:T(8,128)(2,1)} copy(bf16[2,256,2,24,64]{1,4,3,2,0:T(8,128)(2,1)S(1)} %bitcast.99) | data formatting | bytes 6291456 | tf_op jit(solution)/shard_map/reshape | solution.py:105
  322.9 40.2 %all_to_all.63 = bf16[4,2,196608]{2,1,0:T(2,128)(2,1)} all-to-all(bf16[4,2,196608]{2,1,0:T(2,128)(2,1)S(1)} %reshape.122), channel_id=1, replica_groups=mesh['row'=4,'col'=8] {'row'}, dimensions={0} | all-to-all | bytes 6291456 | tf_op jit(solution)/shard_map/all_to_all | solution.py:106
  363.2 7.6 %reshape.123 = bf16[256,2,2,24,64]{4,3,2,1,0:T(8,128)(2,1)} reshape(bf16[4,2,196608]{2,1,0:T(2,128)(2,1)} %all_to_all.63) | data formatting | bytes 6291456
  370.7 10.2 %copy.46 = bf16[2,4,64,2,24,64]{5,1,2,4,3,0:T(4,128)(2,1)} copy(bf16[2,4,64,2,24,64]{5,4,3,0,2,1:T(8,128)(2,1)} %bitcast.91) | data formatting | bytes 6291456 | tf_op jit(solution)/shard_map/all_to_all | solution.py:106
  381.0 8.9 %all_to_all.55 = bf16[2,64,2,24,256]{4,1,3,2,0:T(8,128)(2,1)S(1)} reshape(bf16[2,64,2,24,4,64]{5,4,1,3,2,0:T(4,128)(2,1)} %bitcast.92) | data formatting | bytes 6291456 | tf_op jit(solution)/shard_map/all_to_all | solution.py:106
  401.2 14.4 %copy.35 = bf16[2,384,64,48]{2,3,0,1:T(8,128)(2,1)} copy(bf16[2,384,64,48]{1,2,3,0:T(8,128)(2,1)} %bitcast.93) | data formatting | bytes 9437184 | tf_op jit(solution)/shard_map/convert_element_type | solution.py:111
  415.7 11.3 %reshape.124 = bf16[8,2,147456]{2,1,0:T(2,128)(2,1)} reshape(bf16[384,2,48,64]{3,2,1,0:T(8,128)(2,1)} %bitcast.84) | data formatting | bytes 9437184
  427.0 109.0 %all_to_all.64 = bf16[8,2,147456]{2,1,0:T(2,128)(2,1)} all-to-all(bf16[8,2,147456]{2,1,0:T(2,128)(2,1)} %reshape.124), channel_id=1, replica_groups=mesh['row'=4,'col'=8] {'col'}, dimensions={0} | all-to-all | bytes 9437184 | tf_op jit(solution)/shard_map/all_to_all | solution.py:113
  536.1 11.2 %reshape.125 = bf16[384,2,48,64]{3,2,1,0:T(8,128)(2,1)} reshape(bf16[8,2,147456]{2,1,0:T(2,128)(2,1)} %all_to_all.64) | data formatting | bytes 9437184
  547.2 11.0 %copy.37 = bf16[2,48,64,8,48]{2,1,0,4,3:T(8,128)(2,1)} copy(bf16[2,48,64,8,48]{2,4,0,1,3:T(8,128)(2,1)} %bitcast.85) | data formatting | bytes 9437184 | tf_op jit(solution)/shard_map/all_to_all | solution.py:113
  558.2 13.0 %reshape.113 = bf16[6144,384]{0,1:T(8,128)(2,1)} reshape(bf16[2,48,64,8,48]{2,1,0,4,3:T(8,128)(2,1)} %copy.37) | data formatting | bytes 9437184 | tf_op jit(solution)/shard_map/reshape | solution.py:114
  571.3 7.9 %convolution_convert_fusion = bf16[6144,384]{1,0:T(8,128)(2,1)S(1)} fusion(bf16[6144,384]{0,1:T(8,128)(2,1)} %reshape.113, s32[384]{0:T(512)S(1)} %get-tuple-element.14, s32[384]{0:T(512)S(1)} %get-tuple-element.15, s32[384]{0:T(512)S(1)} %get-tuple-element.12, s32[384]{0:T(512)S(1)} %get-tuple-element.18, s32[384]{0:T(512)S(1)} %get-tuple-element.13, ...), kind=kOutput, calls=%fused_computation | convolution fusion | flops 1819312128 | bytes 9447552 | tf_op jit(solution)/shard_map/dot_general | solution.py:114
  (50 shorter events, 65.8 us)
Async XLA Ops:
  0.6 300.1 %copy-start = (bf16[256,256]{1,0:T(8,128)(2,1)S(1)}, bf16[256,256]{1,0:T(8,128)(2,1)}, u32[]{:S(2)}) copy-start(bf16[256,256]{1,0:T(8,128)(2,1)} %param.7) | copy-start | bytes 393220
  36.7 112.0 %all-to-all-start = ((bf16[8,2,147456]{2,1,0:T(2,128)(2,1)}), bf16[8,2,147456]{2,1,0:T(2,128)(2,1)}, u32[]{:S(2)}, u32[]{:S(2)}) async-start(bf16[8,2,147456]{2,1,0:T(2,128)(2,1)} %reshape.118), calls=%async_computation | async-start | bytes 9437184 | tf_op jit(solution)/shard_map/all_to_all | solution.py:76
  206.4 5.8 %slice-start = ((s8[4718592]{0:T(1024)(128)(4,1)}), s8[4194304]{0:T(1024)(128)(4,1)S(1)}, s32[]{:S(2)}) async-start(s8[4718592]{0:T(1024)(128)(4,1)} %bitcast.80), calls=%async_computation.4 | async-start | bytes 8388608
  206.4 5.9 %slice-start.1 = ((s8[4718592]{0:T(1024)(128)(4,1)}), s8[524288]{0:T(1024)(128)(4,1)S(1)}, s32[]{:S(2)}) async-start(s8[4718592]{0:T(1024)(128)(4,1)} %bitcast.80), calls=%async_computation.5 | async-start | bytes 1048576
  235.6 4.4 copy-start.4
  235.6 40.9 %all-to-all-start.1 = ((bf16[4,2,196608]{2,1,0:T(2,128)(2,1)}), bf16[4,2,196608]{2,1,0:T(2,128)(2,1)S(1)}, u32[]{:S(2)}, u32[]{:S(2)}) async-start(bf16[4,2,196608]{2,1,0:T(2,128)(2,1)} %reshape.120), calls=%async_computation.1 | async-start | bytes 6291456 | tf_op jit(solution)/shard_map/all_to_all | solution.py:86
  300.8 1.4 copy-start.3
  301.8 1.5 copy-start.2
  303.7 1.3 copy-start.5
  571.2 10.5 %copy-start.1 = (bf16[256,256]{1,0:T(8,128)(2,1)S(1)}, bf16[256,256]{1,0:T(8,128)(2,1)}, u32[]{:S(2)}) copy-start(bf16[256,256]{1,0:T(8,128)(2,1)} %param.7) | copy-start | bytes 393220
where the time goes:
time: 589 us; the launch traced here: 582 us
  local copies, waits for them, and re-layouts  235 us (40%)
  blocking collectives  149 us (25%)
  waiting for transfers between devices  139 us (24%)
  matrix products  33.5 us (6%)
  other arithmetic  12.6 us (2%)
  starting transfers between devices  11.6 us (2%)
    all_to_all x1, blocking collectives, shards(): lax.all_to_all(zlines, 'col', split_axis=1, concat_axis=3, tiled=True)  109 us
    all_to_all x1, waiting for transfers between devices, shards(): lax.all_to_all(spectra, 'col', split_axis=3, concat_axis=1, tiled=True)  104 us
    unnamed x24, local copies, waits for them, and re-layouts  73.7 us
    all_to_all x1, blocking collectives, shards(): lax.all_to_all(solved, 'row', split_axis=1, concat_axis=4, tiled=True)  40.2 us
    all_to_all x1, waiting for transfers between devices, shards(): lax.all_to_all(zmodes, 'row', split_axis=4, concat_axis=1, tiled=True)  34.6 us
    reshape x1, local copies, waits for them, and re-layouts, shards(): flat = block.reshape(2, depth, -1)  23.8 us
    all_to_all x2, local copies, waits for them, and re-layouts, shards(): lax.all_to_all(solved, 'row', split_axis=1, concat_axis=4, tiled=True)  19.1 us
    all_to_all x1, local copies, waits for them, and re-layouts, shards(): lax.all_to_all(spectra, 'col', split_axis=3, concat_axis=1, tiled=True)  16.2 us
  transfers between devices with their start and end apart: 2, of which 2 were waited for; matrix products, arithmetic and copies ran while one was open for 0% of the time, Pallas kernels for 0%

commit v1 on v0

--- a/solution.py
+++ b/solution.py
@@ -1,11 +1,17 @@
+import functools
 import math
 
 import jax
 import jax.numpy as jnp
+import numpy as np
 from jax import lax
+from jax.experimental import pallas as pl
+from jax.experimental.pallas import tpu as pltpu
 from jax.sharding import PartitionSpec as P
 
 KEEP = 256
+CHUNKS = 3
+MESH = pl.DeviceIdType.MESH
 
 
 diffusion = 0.5
@@ -116,12 +122,330 @@
     return (result[0], result[1])
 
 
+def flip(at, d):
+    moved = at
+    for bit in range(d.bit_length()):
+        step = 1 << bit
+        if d & step:
+            moved = moved + (1 - 2 * ((at // step) % 2)) * step
+    return moved
+
+
+def order(n):
+    return list(range(n - 1, 0, -1))
+
+
+def transform_kernel(
+    dims, f0, f1, tab, gf, gi, wf, wb, rates, hout,
+    tmp, send1, recv1, bsend, brecv, esend, erecv, hsend,
+    s1s, s1r, s1l, s2s, s2r, s2l, s3s, s3r, s3l, s4s, s4r, s4l,
+):
+    cols, rows, chunks, mc, zl, yl, height, depth, width = dims
+    nl = KEEP // rows
+    per = mc * chunks
+    lanes = 2 * yl
+    qc = 2 * mc
+    col_at = lax.axis_index("col")
+    row_at = lax.axis_index("row")
+
+    barrier = pltpu.get_barrier_semaphore()
+    for d in range(1, cols):
+        pl.semaphore_signal(barrier, inc=1, device_id={"col": flip(col_at, d)}, device_id_type=MESH)
+    for d in range(1, rows):
+        pl.semaphore_signal(barrier, inc=1, device_id={"row": flip(row_at, d)}, device_id_type=MESH)
+    pl.semaphore_wait(barrier, cols + rows - 2)
+
+    def exchange(axis, n, at, src, dst, ss, rs, ls, k):
+        own = pltpu.make_async_copy(src(at), dst(at), ls.at[k])
+        pairs = []
+        for d in order(n):
+            peer = flip(at, d)
+            pairs.append(
+                pltpu.make_async_remote_copy(
+                    src_ref=src(peer),
+                    dst_ref=dst(at),
+                    send_sem=ss.at[k, d],
+                    recv_sem=rs.at[k, d],
+                    device_id={axis: peer},
+                    device_id_type=MESH,
+                )
+            )
+        return own, pairs
+
+    def ex1(k):
+        return exchange(
+            "col", cols, col_at,
+            lambda p: send1.at[k, pl.ds(p * qc, qc)],
+            lambda p: recv1.at[k, :, pl.ds(pl.multiple_of(p * zl, 16), zl), :],
+            s1s, s1r, s1l, k,
+        )
+
+    def ex2(k):
+        return exchange(
+            "row", rows, row_at,
+            lambda p: bsend.at[k, :, :, pl.ds(pl.multiple_of(p * nl, 16), nl), :],
+            lambda p: brecv.at[k, p],
+            s2s, s2r, s2l, k,
+        )
+
+    def ex3(k):
+        return exchange(
+            "row", rows, row_at,
+            lambda p: esend.at[k, p],
+            lambda p: erecv.at[k, :, :, pl.ds(pl.multiple_of(p * nl, 16), nl), :],
+            s3s, s3r, s3l, k,
+        )
+
+    def ex4(k):
+        return exchange(
+            "col", cols, col_at,
+            lambda p: hsend.at[k, :, :, pl.ds(pl.multiple_of(p * zl, 16), zl), :],
+            lambda p: hout.at[k, p],
+            s4s, s4r, s4l, k,
+        )
+
+    def begin(ex):
+        own, pairs = ex
+        for c in pairs:
+            c.start()
+        own.start()
+
+    def arrive(ex):
+        own, pairs = ex
+        own.wait()
+        for c in pairs:
+            c.wait_recv()
+
+    def leave(ex):
+        for c in ex[1]:
+            c.wait_send()
+
+    def forward(k, carry):
+        def block(zb, carry):
+            for zi in range(0, 16, 2):
+                z = zb * 16 + zi
+                lines = jnp.concatenate((f0[z], f1[z], f0[z + 1], f1[z + 1]), axis=0)
+                acc = lax.dot_general(
+                    tab[k], lines, (((1,), (1,)), ((), ())), preferred_element_type=jnp.float32
+                )
+                tmp[:, zi, :] = acc[:, :lanes]
+                tmp[:, zi + 1, :] = acc[:, lanes:]
+            at = pl.multiple_of(zb * 16, 16)
+            send1[k, :, pl.ds(at, 16), :] = tmp[...].astype(jnp.bfloat16)
+            return carry
+
+        lax.fori_loop(0, zl // 16, block, 0)
+        begin(ex1(k))
+        return carry
+
+    lax.fori_loop(0, chunks, forward, 0)
+
+    def zforward(k):
+        def pair(i, carry):
+            m = 2 * i
+            x = jnp.concatenate(
+                [
+                    jnp.concatenate((recv1[k, m + a], recv1[k, mc + m + a]), axis=0)
+                    for a in range(2)
+                ],
+                axis=1,
+            )
+            b = jnp.dot(gf[...], x, preferred_element_type=jnp.float32).astype(jnp.bfloat16)
+            for a in range(2):
+                for p in range(2):
+                    bsend[k, m + a, p] = b[p * KEEP:(p + 1) * KEEP, a * lanes:(a + 1) * lanes]
+            return carry
+
+        lax.fori_loop(0, mc // 2, pair, 0)
+
+    def solve(k):
+        n = row_at * nl + lax.broadcasted_iota(jnp.int32, (nl, 1), 0)
+        n = jnp.where(n < KEEP // 2, n, n + (depth - KEEP))
+        n = jnp.where(n < depth // 2, n, n - depth)
+        kz_sq = (n.astype(jnp.float32) * (2.0 * math.pi / depth)) ** 2
+
+        def one(m, carry):
+            mode = jnp.full((1, 1), col_at * per + k * mc + m, jnp.int32)
+            kx_sq = (mode.astype(jnp.float32) * (2.0 * math.pi / width)) ** 2
+            total = (kx_sq + kz_sq) + rates[...]
+            field = lax.broadcasted_iota(jnp.int32, total.shape, 1) // height
+            inv = 1.0 / jnp.where(field == 0, -total, 1.0 + diffusion * total)
+            line = jnp.concatenate(
+                [brecv[k, s, m].reshape(2 * nl, lanes) for s in range(rows)], axis=1
+            )
+            c = jnp.dot(line, wf[...], preferred_element_type=jnp.float32)
+            hat = (c * jnp.concatenate((inv, inv), axis=0)).astype(jnp.bfloat16)
+            e = jnp.dot(hat, wb[...], preferred_element_type=jnp.float32).astype(jnp.bfloat16)
+            for r in range(rows):
+                esend[k, r, m] = e[:, r * lanes:(r + 1) * lanes].reshape(2, nl, lanes)
+            return carry
+
+        lax.fori_loop(0, mc, one, 0)
+
+    def zback(k):
+        def pair(i, carry):
+            m = 2 * i
+            x = jnp.concatenate(
+                [erecv[k, m + a].reshape(2 * KEEP, lanes) for a in range(2)], axis=1
+            )
+            h = jnp.dot(gi[...], x, preferred_element_type=jnp.float32).astype(jnp.bfloat16)
+            for a in range(2):
+                for p in range(2):
+                    hsend[k, p, m + a] = h[p * depth:(p + 1) * depth, a * lanes:(a + 1) * lanes]
+            return carry
+
+        lax.fori_loop(0, mc // 2, pair, 0)
+
+    def middle(k, carry):
+        arrive(ex1(k))
+        zforward(k)
+        begin(ex2(k))
+        arrive(ex2(k))
+        solve(k)
+        begin(ex3(k))
+        arrive(ex3(k))
+        zback(k)
+        begin(ex4(k))
+        return carry
+
+    lax.fori_loop(0, chunks, middle, 0)
+
+    def finish(k, carry):
+        leave(ex1(k))
+        leave(ex2(k))
+        leave(ex3(k))
+        leave(ex4(k))
+        arrive(ex4(k))
+        return carry
+
+    lax.fori_loop(0, chunks, finish, 0)
+
+
+def back_kernel(yl, h, bx, o0, o1, tmp):
+    lines = tmp.shape[0]
+    lanes = 2 * yl
+    tmp[...] = h[...].reshape(tmp.shape).astype(jnp.float32)
+    for zi in range(0, tmp.shape[1], 2):
+        x = jnp.concatenate((tmp[:, zi, :], tmp[:, zi + 1, :]), axis=1).astype(jnp.bfloat16)
+        out = lax.dot_general(
+            x, bx[...], (((0,), (0,)), ((), ())), preferred_element_type=jnp.float32
+        ).astype(jnp.bfloat16)
+        o0[zi] = out[:yl]
+        o1[zi] = out[yl:lanes]
+        o0[zi + 1] = out[lanes:lanes + yl]
+        o1[zi + 1] = out[lanes + yl:]
+
+
+def tables(cols, chunks, mc, depth, width):
+    per = mc * chunks
+    mode = np.arange(width // 2).reshape(cols, chunks, mc)
+    mode = np.stack((mode, mode), axis=2).transpose(1, 0, 2, 3).reshape(-1)
+    part = np.broadcast_to(np.arange(2)[None, None, :, None], (chunks, cols, 2, mc)).reshape(-1)
+    place = np.arange(width)
+    angle = (mode[:, None] * place[None, :] % width).astype(np.float32) * np.float32(
+        2.0 * math.pi / width
+    )
+    factor = np.float32(math.sqrt(2.0 / width))
+    wave_x = np.where(part[:, None] == 0, factor * np.cos(angle), -factor * np.sin(angle))
+    weight = np.where(mode == 0, 0.5, 1.0).astype(np.float32)[:, None]
+    tab = wave_x.astype(jnp.bfloat16).reshape(chunks, -1, width)
+    back = (wave_x * weight).astype(jnp.bfloat16)
+    wave = np.arange(KEEP)
+    wave = np.where(wave < KEEP // 2, wave, wave + (depth - KEEP))
+    angle = (wave[:, None] * np.arange(depth)[None, :] % depth).astype(np.float32) * np.float32(
+        2.0 * math.pi / depth
+    )
+    factor = np.float32(1.0 / math.sqrt(depth))
+    c, s = factor * np.cos(angle), factor * np.sin(angle)
+    gf = np.block([[c, s], [-s, c]]).astype(jnp.bfloat16)
+    gi = np.block([[c.T, -s.T], [s.T, c.T]]).astype(jnp.bfloat16)
+    return tab, back, gf, gi
+
+
+def fused(pressure_rhs, scalar_source, forward_y, back_y, wall_rates):
+    rows = lax.axis_size("row")
+    cols = lax.axis_size("col")
+    zl, yl, width = pressure_rhs.shape
+    height = forward_y.shape[0]
+    depth = zl * cols
+    per = width // (2 * cols)
+    chunks = CHUNKS
+    mc = per // chunks
+    nl = KEEP // rows
+    lanes = 2 * yl
+    tab, back, gf, gi = tables(cols, chunks, mc, depth, width)
+    eye = jnp.eye(2, dtype=jnp.bfloat16)
+    wf = forward_y.T.reshape(rows, 1, yl, 1, height) * eye.reshape(1, 2, 1, 2, 1)
+    wf = wf.reshape(rows * lanes, 2 * height)
+    wb = back_y.T.reshape(1, height, rows, 1, yl) * eye.reshape(2, 1, 1, 2, 1)
+    wb = wb.reshape(2 * height, rows * lanes)
+    rates = jnp.concatenate((wall_rates, wall_rates)).reshape(1, 2 * height)
+    dims = (cols, rows, chunks, mc, zl, yl, height, depth, width)
+    bf = jnp.bfloat16
+    dma = pltpu.SemaphoreType.DMA
+    sems = []
+    for n in (cols, rows, rows, cols):
+        sems += [dma((chunks, n)), dma((chunks, n)), dma((chunks,))]
+    h = pl.pallas_call(
+        functools.partial(transform_kernel, dims),
+        out_shape=jax.ShapeDtypeStruct((chunks, cols, 2, mc, zl, lanes), bf),
+        in_specs=[pl.BlockSpec(memory_space=pltpu.VMEM)] * 8,
+        out_specs=pl.BlockSpec(memory_space=pl.ANY),
+        scratch_shapes=[
+            pltpu.VMEM((cols * 2 * mc, 16, lanes), jnp.float32),
+            pltpu.VMEM((chunks, cols * 2 * mc, zl, lanes), bf),
+            pltpu.VMEM((chunks, 2 * mc, depth, lanes), bf),
+            pltpu.VMEM((chunks, mc, 2, KEEP, lanes), bf),
+            pltpu.VMEM((chunks, rows, mc, 2, nl, lanes), bf),
+            pltpu.VMEM((chunks, rows, mc, 2, nl, lanes), bf),
+            pltpu.VMEM((chunks, mc, 2, KEEP, lanes), bf),
+            pltpu.VMEM((chunks, 2, mc, depth, lanes), bf),
+        ] + sems,
+        compiler_params=pltpu.CompilerParams(
+            collective_id=0, has_side_effects=True, vmem_limit_bytes=56 << 20
+        ),
+    )(pressure_rhs, scalar_source, tab, gf, gi, wf, wb, rates)
+    h = h.reshape(width, zl, lanes)
+    return pl.pallas_call(
+        functools.partial(back_kernel, yl),
+        grid=(zl // 16,),
+        out_shape=[jax.ShapeDtypeStruct((zl, yl, width), bf)] * 2,
+        in_specs=[
+            pl.BlockSpec((width, 16, lanes), lambda i: (0, i, 0)),
+            pl.BlockSpec((width, width), lambda i: (0, 0)),
+        ],
+        out_specs=[pl.BlockSpec((16, yl, width), lambda i: (i, 0, 0))] * 2,
+        scratch_shapes=[pltpu.VMEM((width, 16, lanes), jnp.float32)],
+        compiler_params=pltpu.CompilerParams(vmem_limit_bytes=40 << 20),
+    )(h, back)
+
+
+def fits(rows, cols, pressure_rhs, forward_y):
+    depth, height, width = pressure_rhs.shape
+    power = rows & (rows - 1) == 0 and cols & (cols - 1) == 0
+    if depth % cols or height % rows or width % (2 * cols * CHUNKS) or KEEP % rows:
+        return False
+    return (
+        power
+        and (2 * height // rows) % 128 == 0
+        and (depth // cols) % 16 == 0
+        and (KEEP // rows) % 16 == 0
+        and (width // (2 * cols * CHUNKS)) % 2 == 0
+    )
+
+
 def solution(mesh):
     placed = (P("col", "row", None), P("col", "row", None), P(), P(), P())
-    return jax.shard_map(
-        shards,
-        mesh=mesh,
-        in_specs=placed,
-        out_specs=(P("col", "row", None), P("col", "row", None)),
-        check_vma=False,
-    )
+    rows, cols = mesh.shape["row"], mesh.shape["col"]
+
+    def run(pressure_rhs, scalar_source, forward_y, back_y, wall_rates):
+        body = fused if fits(rows, cols, pressure_rhs, forward_y) else shards
+        return jax.shard_map(
+            body,
+            mesh=mesh,
+            in_specs=placed,
+            out_specs=(P("col", "row", None), P("col", "row", None)),
+            check_vma=False,
+        )(pressure_rhs, scalar_source, forward_y, back_y, wall_rates)
+
+    return run

time: 589 us -> 239 us (0.41)
  local copies, waits for them, and re-layouts: 235 us -> 5.41 us
  Pallas kernels: 0 us -> 228 us
  blocking collectives: 149 us -> 0 us
  waiting for transfers between devices: 139 us -> 0 us
  matrix products: 33.5 us -> 0 us
  starting transfers between devices: 11.6 us -> 0 us
  other arithmetic: 12.6 us -> 3.26 us
    pallas_call x0 -> x2, Pallas kernels: none -> 228 us  [the longest x1 219 us: fused(): pl.pallas_call(functools.partial(transform_kernel, dims), out_shape=jax.S...]
    all_to_all x2 -> x0, blocking collectives: 149 us -> none  [the longest x1 109 us: shards(): lax.all_to_all(zlines, 'col', split_axis=1, concat_axis=3, tiled=True)]
    all_to_all x2 -> x0, waiting for transfers between devices: 139 us -> none  [the longest x1 104 us: shards(): lax.all_to_all(spectra, 'col', split_axis=3, concat_axis=1, tiled=True)]
    reshape x5 -> x0, local copies, waits for them, and re-layouts: 69.5 us -> none  [the longest x1 23.8 us: shards(): flat = block.reshape(2, depth, -1)]
    unnamed x24 -> x7, local copies, waits for them, and re-layouts: 73.7 us -> 4.3 us
    all_to_all x5 -> x0, local copies, waits for them, and re-layouts: 56.6 us -> none  [the longest x2 19.1 us: shards(): lax.all_to_all(solved, 'row', split_axis=1, concat_axis=4, tiled=True)]
    dot_general x8 -> x0, matrix products: 33.5 us -> none  [the longest x1 7.88 us: shards(): jnp.dot(block.reshape(-1, width), back_x, preferred_element_type=jnp.floa...]
    convert_element_type x1, local copies, waits for them, and re-layouts: 14.4 us -> 0.11 us  [fused(): eye = jnp.eye(2, dtype=jnp.bfloat16)]
  transfers between devices with their start and end apart: 2 -> 0, of which waited for: 2 -> 0; matrix products, arithmetic and copies ran while one was open for 0% -> 0% of each run, Pallas kernels for 0% -> 0%
where the time goes in v1:
time: 239 us; the launch traced here: 237 us
  Pallas kernels  228 us (95%)
  local copies, waits for them, and re-layouts  5.41 us (2%)
  other arithmetic  3.26 us (1%)
    pallas_call x1, Pallas kernels, fused(): pl.pallas_call(functools.partial(transform_kernel, dims), out_shape=jax.S...  219 us
    pallas_call x1, Pallas kernels, fused(): pl.pallas_call(functools.partial(back_kernel, yl), grid=(zl // 16,), out_...  8.68 us

profile of v1, /device:TPU:0, one launch (start us, length us, event | category | flops | bytes accessed | tf_op | source)
XLA Modules:
  0.0 237.5 jit_solution(15528130117354584742)
XLA Ops:
  0.6 0.1 copy.14
  0.7 1.3 pad_maximum_fusion
  2.1 1.0 copy.13
  3.1 0.5 broadcast_multiply_fusion.1
  3.6 0.9 copy.16
  4.5 1.4 broadcast_multiply_fusion
  5.9 0.1 copy.17
  6.0 1.0 copy.15.wb
  7.0 0.0 copy-start.1
  7.0 219.4 %shard_map.104 = bf16[3,8,2,8,48,128]{5,4,3,2,1,0:T(8,128)(2,1)} custom-call(bf16[48,64,384]{2,1,0:T(8,128)(2,1)} %f0.1, bf16[48,64,384]{2,1,0:T(8,128)(2,1)} %f1.1, bf16[3,128,384]{2,1,0:T(8,128)(2,1)} %constant.8.clone.tab, bf16[512,768]{1,0:T(8,128)(2,1)} %constant.9.clone.gf, bf16[768,512]{1,0:T(8,128)(2,1)} %constant.10.clone.gi, ...), custom_call_target="tpu_custom_call" | custom-call | tf_op jit(solution)/shard_map/pallas_call | solution.py:389
  226.4 0.0 copy-done.1
  226.5 0.0 copy-start
  226.5 2.3 copy-done
  228.8 8.7 %shard_map.105 = (bf16[48,64,384]{2,1,0:T(8,128)(2,1)}, bf16[48,64,384]{2,1,0:T(8,128)(2,1)}) custom-call(bf16[384,48,128]{2,1,0:T(8,128)(2,1)S(1)} %bitcast.16, bf16[384,384]{1,0:T(8,128)(2,1)S(1)} %copy-done.1), custom_call_target="tpu_custom_call" | custom-call | tf_op jit(solution)/shard_map/pallas_call | solution.py:409
  (1 shorter events, 0.0 us)
Async XLA Ops:
  7.0 219.5 %copy-start.1 = (bf16[384,384]{1,0:T(8,128)(2,1)S(1)}, bf16[384,384]{1,0:T(8,128)(2,1)}, u32[]{:S(2)}) copy-start(bf16[384,384]{1,0:T(8,128)(2,1)} %constant.11.clone.bx) | copy-start | bytes 884740
  226.5 2.3 copy-start

commit v2 on v1

--- a/solution.py
+++ b/solution.py
@@ -136,8 +136,10 @@
 
 
 def transform_kernel(
-    dims, f0, f1, tab, gf, gi, wf, wb, rates, hout,
-    tmp, send1, recv1, bsend, brecv, esend, erecv, hsend,
+    dims, p_hbm, s_hbm, tab_hbm, gf_hbm, gi_hbm, bx_hbm, fy, by, rates, po_hbm, so_hbm,
+    f0, f1, tab, gf, gi, bx, wf, wb,
+    tmp, send1, recv1, bsend, brecv, esend, erecv, hsend, hrecv, acc,
+    in_sem, tab_sem, out_sem,
     s1s, s1r, s1l, s2s, s2r, s2l, s3s, s3r, s3l, s4s, s4r, s4l,
 ):
     cols, rows, chunks, mc, zl, yl, height, depth, width = dims
@@ -145,8 +147,31 @@
     per = mc * chunks
     lanes = 2 * yl
     qc = 2 * mc
+    blocks = zl // 16
     col_at = lax.axis_index("col")
     row_at = lax.axis_index("row")
+
+    def span(zb):
+        return pl.ds(pl.multiple_of(zb * 16, 16), 16)
+
+    def load(field, zb):
+        src, dst = ((p_hbm, f0), (s_hbm, f1))[field]
+        return pltpu.make_async_copy(src.at[span(zb)], dst.at[span(zb)], in_sem.at[field, zb])
+
+    def store(field, zb):
+        src, dst = ((f0, po_hbm), (f1, so_hbm))[field]
+        return pltpu.make_async_copy(src.at[span(zb)], dst.at[span(zb)], out_sem.at[field, zb])
+
+    consts = [
+        pltpu.make_async_copy(src, dst, tab_sem.at[i])
+        for i, (src, dst) in enumerate(((tab_hbm, tab), (gf_hbm, gf), (gi_hbm, gi), (bx_hbm, bx)))
+    ]
+    consts[0].start()
+    for zb in range(blocks):
+        load(0, zb).start()
+        load(1, zb).start()
+    for c in consts[1:]:
+        c.start()
 
     barrier = pltpu.get_barrier_semaphore()
     for d in range(1, cols):
@@ -156,7 +181,7 @@
     pl.semaphore_wait(barrier, cols + rows - 2)
 
     def exchange(axis, n, at, src, dst, ss, rs, ls, k):
-        own = pltpu.make_async_copy(src(at), dst(at), ls.at[k])
+        own = lambda: pltpu.make_async_copy(src(at), dst(at), ls.at[k])
         pairs = []
         for d in order(n):
             peer = flip(at, d)
@@ -172,12 +197,12 @@
             )
         return own, pairs
 
-    def ex1(k):
+    def ex1(k, zb):
         return exchange(
             "col", cols, col_at,
-            lambda p: send1.at[k, pl.ds(p * qc, qc)],
-            lambda p: recv1.at[k, :, pl.ds(pl.multiple_of(p * zl, 16), zl), :],
-            s1s, s1r, s1l, k,
+            lambda p: send1.at[k, pl.ds(p * qc, qc), span(zb), :],
+            lambda p: recv1.at[k, :, pl.ds(pl.multiple_of(p * zl + zb * 16, 16), 16), :],
+            s1s, s1r, s1l, k * blocks + zb,
         )
 
     def ex2(k):
@@ -196,23 +221,23 @@
             s3s, s3r, s3l, k,
         )
 
-    def ex4(k):
+    def ex4(k, zb):
         return exchange(
             "col", cols, col_at,
-            lambda p: hsend.at[k, :, :, pl.ds(pl.multiple_of(p * zl, 16), zl), :],
-            lambda p: hout.at[k, p],
-            s4s, s4r, s4l, k,
+            lambda p: hsend.at[k, :, :, pl.ds(pl.multiple_of(p * zl + zb * 16, 16), 16), :],
+            lambda p: hrecv.at[k, p, :, :, span(zb), :],
+            s4s, s4r, s4l, k * blocks + zb,
         )
 
     def begin(ex):
         own, pairs = ex
         for c in pairs:
             c.start()
-        own.start()
+        own().start()
 
     def arrive(ex):
         own, pairs = ex
-        own.wait()
+        own().wait()
         for c in pairs:
             c.wait_recv()
 
@@ -220,25 +245,45 @@
         for c in ex[1]:
             c.wait_send()
 
-    def forward(k, carry):
-        def block(zb, carry):
-            for zi in range(0, 16, 2):
-                z = zb * 16 + zi
-                lines = jnp.concatenate((f0[z], f1[z], f0[z + 1], f1[z + 1]), axis=0)
-                acc = lax.dot_general(
-                    tab[k], lines, (((1,), (1,)), ((), ())), preferred_element_type=jnp.float32
-                )
-                tmp[:, zi, :] = acc[:, :lanes]
-                tmp[:, zi + 1, :] = acc[:, lanes:]
-            at = pl.multiple_of(zb * 16, 16)
-            send1[k, :, pl.ds(at, 16), :] = tmp[...].astype(jnp.bfloat16)
-            return carry
-
-        lax.fori_loop(0, zl // 16, block, 0)
-        begin(ex1(k))
+    consts[0].wait()
+
+    def forward(i, carry):
+        k, zb = i // blocks, i % blocks
+
+        @pl.when(k == 0)
+        def _():
+            load(0, zb).wait()
+            load(1, zb).wait()
+
+        for zi in range(0, 16, 2):
+            z = zb * 16 + zi
+            lines = jnp.concatenate((f0[z], f1[z], f0[z + 1], f1[z + 1]), axis=0)
+            out = lax.dot_general(
+                tab[k], lines, (((1,), (1,)), ((), ())), preferred_element_type=jnp.float32
+            )
+            tmp[:, zi, :] = out[:, :lanes]
+            tmp[:, zi + 1, :] = out[:, lanes:]
+        send1[k, :, span(zb), :] = tmp[...].astype(jnp.bfloat16)
+        begin(ex1(k, zb))
         return carry
 
-    lax.fori_loop(0, chunks, forward, 0)
+    lax.fori_loop(0, chunks * blocks, forward, 0)
+    for c in consts[1:]:
+        c.wait()
+
+    wf[...] = jnp.zeros_like(wf)
+    lines = fy[...].T
+    for s in range(rows):
+        for f in range(2):
+            wf[s * lanes + f * yl:s * lanes + (f + 1) * yl, f * height:(f + 1) * height] = lines[
+                s * yl:(s + 1) * yl
+            ]
+    lines = by[...].T
+    blank = jnp.zeros((height, yl), jnp.bfloat16)
+    for r in range(rows):
+        part = lines[:, r * yl:(r + 1) * yl]
+        wb[:height, r * lanes:(r + 1) * lanes] = jnp.concatenate((part, blank), axis=1)
+        wb[height:, r * lanes:(r + 1) * lanes] = jnp.concatenate((blank, part), axis=1)
 
     def zforward(k):
         def pair(i, carry):
@@ -267,7 +312,7 @@
         def one(m, carry):
             mode = jnp.full((1, 1), col_at * per + k * mc + m, jnp.int32)
             kx_sq = (mode.astype(jnp.float32) * (2.0 * math.pi / width)) ** 2
-            total = (kx_sq + kz_sq) + rates[...]
+            total = (kx_sq + kz_sq) + jnp.concatenate((rates[...], rates[...]), axis=1)
             field = lax.broadcasted_iota(jnp.int32, total.shape, 1) // height
             inv = 1.0 / jnp.where(field == 0, -total, 1.0 + diffusion * total)
             line = jnp.concatenate(
@@ -296,8 +341,15 @@
 
         lax.fori_loop(0, mc // 2, pair, 0)
 
+    def each(k, act):
+        def one(zb, carry):
+            act(k, zb)
+            return carry
+
+        lax.fori_loop(0, blocks, one, 0)
+
     def middle(k, carry):
-        arrive(ex1(k))
+        each(k, lambda k, zb: arrive(ex1(k, zb)))
         zforward(k)
         begin(ex2(k))
         arrive(ex2(k))
@@ -305,35 +357,47 @@
         begin(ex3(k))
         arrive(ex3(k))
         zback(k)
-        begin(ex4(k))
+        each(k, lambda k, zb: begin(ex4(k, zb)))
         return carry
 
     lax.fori_loop(0, chunks, middle, 0)
 
+    def result(k, zb):
+        arrive(ex4(k, zb))
+        tmp[...] = hrecv[k, :, :, :, span(zb), :].reshape(tmp.shape).astype(jnp.float32)
+        for zi in range(0, 16, 2):
+            z = zb * 16 + zi
+            x = jnp.concatenate((tmp[:, zi, :], tmp[:, zi + 1, :]), axis=1).astype(jnp.bfloat16)
+            out = lax.dot_general(
+                x, bx[k], (((0,), (0,)), ((), ())), preferred_element_type=jnp.float32
+            )
+            for a in range(2):
+                half = out[a * lanes:(a + 1) * lanes]
+                if k > 0:
+                    half = acc[z + a] + half
+                if k < chunks - 1:
+                    acc[z + a] = half
+                else:
+                    f0[z + a] = half[:yl].astype(jnp.bfloat16)
+                    f1[z + a] = half[yl:].astype(jnp.bfloat16)
+        if k == chunks - 1:
+            store(0, zb).start()
+            store(1, zb).start()
+
+    for k in range(chunks):
+        each(k, result)
+
     def finish(k, carry):
-        leave(ex1(k))
+        each(k, lambda k, zb: leave(ex1(k, zb)))
         leave(ex2(k))
         leave(ex3(k))
-        leave(ex4(k))
-        arrive(ex4(k))
+        each(k, lambda k, zb: leave(ex4(k, zb)))
         return carry
 
     lax.fori_loop(0, chunks, finish, 0)
-
-
-def back_kernel(yl, h, bx, o0, o1, tmp):
-    lines = tmp.shape[0]
-    lanes = 2 * yl
-    tmp[...] = h[...].reshape(tmp.shape).astype(jnp.float32)
-    for zi in range(0, tmp.shape[1], 2):
-        x = jnp.concatenate((tmp[:, zi, :], tmp[:, zi + 1, :]), axis=1).astype(jnp.bfloat16)
-        out = lax.dot_general(
-            x, bx[...], (((0,), (0,)), ((), ())), preferred_element_type=jnp.float32
-        ).astype(jnp.bfloat16)
-        o0[zi] = out[:yl]
-        o1[zi] = out[yl:lanes]
-        o0[zi + 1] = out[lanes:lanes + yl]
-        o1[zi + 1] = out[lanes + yl:]
+    for zb in range(blocks):
+        store(0, zb).wait()
+        store(1, zb).wait()
 
 
 def tables(cols, chunks, mc, depth, width):
@@ -349,7 +413,7 @@
     wave_x = np.where(part[:, None] == 0, factor * np.cos(angle), -factor * np.sin(angle))
     weight = np.where(mode == 0, 0.5, 1.0).astype(np.float32)[:, None]
     tab = wave_x.astype(jnp.bfloat16).reshape(chunks, -1, width)
-    back = (wave_x * weight).astype(jnp.bfloat16)
+    back = (wave_x * weight).astype(jnp.bfloat16).reshape(chunks, -1, width)
     wave = np.arange(KEEP)
     wave = np.where(wave < KEEP // 2, wave, wave + (depth - KEEP))
     angle = (wave[:, None] * np.arange(depth)[None, :] % depth).astype(np.float32) * np.float32(
@@ -374,50 +438,49 @@
     nl = KEEP // rows
     lanes = 2 * yl
     tab, back, gf, gi = tables(cols, chunks, mc, depth, width)
-    eye = jnp.eye(2, dtype=jnp.bfloat16)
-    wf = forward_y.T.reshape(rows, 1, yl, 1, height) * eye.reshape(1, 2, 1, 2, 1)
-    wf = wf.reshape(rows * lanes, 2 * height)
-    wb = back_y.T.reshape(1, height, rows, 1, yl) * eye.reshape(2, 1, 1, 2, 1)
-    wb = wb.reshape(2 * height, rows * lanes)
-    rates = jnp.concatenate((wall_rates, wall_rates)).reshape(1, 2 * height)
+    rates = wall_rates.reshape(1, height)
     dims = (cols, rows, chunks, mc, zl, yl, height, depth, width)
     bf = jnp.bfloat16
     dma = pltpu.SemaphoreType.DMA
-    sems = []
-    for n in (cols, rows, rows, cols):
-        sems += [dma((chunks, n)), dma((chunks, n)), dma((chunks,))]
-    h = pl.pallas_call(
-        functools.partial(transform_kernel, dims),
-        out_shape=jax.ShapeDtypeStruct((chunks, cols, 2, mc, zl, lanes), bf),
-        in_specs=[pl.BlockSpec(memory_space=pltpu.VMEM)] * 8,
-        out_specs=pl.BlockSpec(memory_space=pl.ANY),
-        scratch_shapes=[
-            pltpu.VMEM((cols * 2 * mc, 16, lanes), jnp.float32),
-            pltpu.VMEM((chunks, cols * 2 * mc, zl, lanes), bf),
-            pltpu.VMEM((chunks, 2 * mc, depth, lanes), bf),
-            pltpu.VMEM((chunks, mc, 2, KEEP, lanes), bf),
-            pltpu.VMEM((chunks, rows, mc, 2, nl, lanes), bf),
-            pltpu.VMEM((chunks, rows, mc, 2, nl, lanes), bf),
-            pltpu.VMEM((chunks, mc, 2, KEEP, lanes), bf),
-            pltpu.VMEM((chunks, 2, mc, depth, lanes), bf),
-        ] + sems,
-        compiler_params=pltpu.CompilerParams(
-            collective_id=0, has_side_effects=True, vmem_limit_bytes=56 << 20
-        ),
-    )(pressure_rhs, scalar_source, tab, gf, gi, wf, wb, rates)
-    h = h.reshape(width, zl, lanes)
-    return pl.pallas_call(
-        functools.partial(back_kernel, yl),
-        grid=(zl // 16,),
-        out_shape=[jax.ShapeDtypeStruct((zl, yl, width), bf)] * 2,
-        in_specs=[
-            pl.BlockSpec((width, 16, lanes), lambda i: (0, i, 0)),
-            pl.BlockSpec((width, width), lambda i: (0, 0)),
-        ],
-        out_specs=[pl.BlockSpec((16, yl, width), lambda i: (i, 0, 0))] * 2,
-        scratch_shapes=[pltpu.VMEM((width, 16, lanes), jnp.float32)],
-        compiler_params=pltpu.CompilerParams(vmem_limit_bytes=40 << 20),
-    )(h, back)
+    blocks = zl // 16
+    sems = [dma((2, blocks)), dma((4,)), dma((2, blocks))]
+    for n, steps in ((cols, chunks * blocks), (rows, chunks), (rows, chunks), (cols, chunks * blocks)):
+        sems += [dma((steps, n)), dma((steps, n)), dma((steps,))]
+    field = jax.ShapeDtypeStruct((zl, yl, width), bf)
+    anywhere = pl.BlockSpec(memory_space=pl.ANY)
+    inside = pl.BlockSpec(memory_space=pltpu.VMEM)
+    vmem = [
+        (field.shape, bf),
+        (field.shape, bf),
+        (tab.shape, bf),
+        (gf.shape, bf),
+        (gi.shape, bf),
+        (back.shape, bf),
+        ((rows * lanes, 2 * height), bf),
+        ((2 * height, rows * lanes), bf),
+        ((cols * 2 * mc, 16, lanes), jnp.float32),
+        ((chunks, cols * 2 * mc, zl, lanes), bf),
+        ((chunks, 2 * mc, depth, lanes), bf),
+        ((chunks, mc, 2, KEEP, lanes), bf),
+        ((chunks, rows, mc, 2, nl, lanes), bf),
+        ((chunks, rows, mc, 2, nl, lanes), bf),
+        ((chunks, mc, 2, KEEP, lanes), bf),
+        ((chunks, 2, mc, depth, lanes), bf),
+        ((chunks, cols, 2, mc, zl, lanes), bf),
+        ((zl, lanes, width), jnp.float32),
+    ]
+    return tuple(
+        pl.pallas_call(
+            functools.partial(transform_kernel, dims),
+            out_shape=[field, field],
+            in_specs=[anywhere] * 6 + [inside] * 3,
+            out_specs=[anywhere] * 2,
+            scratch_shapes=[pltpu.VMEM(*v) for v in vmem] + sems,
+            compiler_params=pltpu.CompilerParams(
+                collective_id=0, has_side_effects=True, vmem_limit_bytes=67043328
+            ),
+        )(pressure_rhs, scalar_source, tab, gf, gi, back, forward_y, back_y, rates)
+    )
 
 
 def fits(rows, cols, pressure_rhs, forward_y):

time: 239 us -> 223 us (0.933)
  Pallas kernels: 228 us -> 217 us
  other arithmetic: 3.26 us -> 0 us
    pallas_call x2 -> x1, Pallas kernels: 228 us -> 217 us  [fused(): pl.pallas_call(functools.partial(transform_kernel, dims), out_shape=[fiel...]
    unnamed x7 -> x4, local copies, waits for them, and re-layouts: 4.3 us -> 4.87 us
where the time goes in v2:
time: 223 us; the launch traced here: 222 us
  Pallas kernels  217 us (97%)
  local copies, waits for them, and re-layouts  4.87 us (2%)
    pallas_call x1, Pallas kernels, fused(): pl.pallas_call(functools.partial(transform_kernel, dims), out_shape=[fiel...  217 us
    unnamed x4, local copies, waits for them, and re-layouts  4.87 us

profile of v2, /device:TPU:0, one launch (start us, length us, event | category | flops | bytes accessed | tf_op | source)
XLA Modules:
  0.0 222.4 jit_solution(17690311968647570955)
XLA Ops:
  0.6 216.9 %shard_map.104 = (bf16[48,64,384]{2,1,0:T(8,128)(2,1)}, bf16[48,64,384]{2,1,0:T(8,128)(2,1)}) custom-call(bf16[48,64,384]{2,1,0:T(8,128)(2,1)} %p_hbm.1, bf16[48,64,384]{2,1,0:T(8,128)(2,1)} %s_hbm.1, bf16[3,128,384]{2,1,0:T(8,128)(2,1)} %constant.8.clone.tab_hbm, bf16[512,768]{1,0:T(8,128)(2,1)} %constant.9.clone.gf_hbm, ...), custom_call_target="tpu_custom_call" | custom-call | tf_op jit(solution)/shard_map/pallas_call | solution.py:473
  217.5 0.0 copy-start
  217.5 3.5 %copy.13 = bf16[48,64,384]{2,1,0:T(8,128)(2,1)} copy(bf16[48,64,384]{2,1,0:T(8,128)(2,1)} %get-tuple-element.4) | data formatting | bytes 4718592
  221.0 0.0 copy-done
  221.0 1.4 copy.14
Async XLA Ops:
  217.5 3.5 %copy-start = (bf16[48,64,384]{2,1,0:T(8,128)(2,1)S(1)}, bf16[48,64,384]{2,1,0:T(8,128)(2,1)}, u32[]{:S(2)}) copy-start(bf16[48,64,384]{2,1,0:T(8,128)(2,1)} %get-tuple-element.5) | copy-start | bytes 7077892

commit v3 on v2

--- a/solution.py
+++ b/solution.py
@@ -136,10 +136,10 @@
 
 
 def transform_kernel(
-    dims, p_hbm, s_hbm, tab_hbm, gf_hbm, gi_hbm, bx_hbm, fy, by, rates, po_hbm, so_hbm,
+    dims, p_hbm, s_hbm, tab_hbm, gf_hbm, gi_hbm, bx_hbm, fy, by, rates, o0, o1,
     f0, f1, tab, gf, gi, bx, wf, wb,
     tmp, send1, recv1, bsend, brecv, esend, erecv, hsend, hrecv, acc,
-    in_sem, tab_sem, out_sem,
+    in_sem, tab_sem,
     s1s, s1r, s1l, s2s, s2r, s2l, s3s, s3r, s3l, s4s, s4r, s4l,
 ):
     cols, rows, chunks, mc, zl, yl, height, depth, width = dims
@@ -157,10 +157,6 @@
     def load(field, zb):
         src, dst = ((p_hbm, f0), (s_hbm, f1))[field]
         return pltpu.make_async_copy(src.at[span(zb)], dst.at[span(zb)], in_sem.at[field, zb])
-
-    def store(field, zb):
-        src, dst = ((f0, po_hbm), (f1, so_hbm))[field]
-        return pltpu.make_async_copy(src.at[span(zb)], dst.at[span(zb)], out_sem.at[field, zb])
 
     consts = [
         pltpu.make_async_copy(src, dst, tab_sem.at[i])
@@ -378,11 +374,8 @@
                 if k < chunks - 1:
                     acc[z + a] = half
                 else:
-                    f0[z + a] = half[:yl].astype(jnp.bfloat16)
-                    f1[z + a] = half[yl:].astype(jnp.bfloat16)
-        if k == chunks - 1:
-            store(0, zb).start()
-            store(1, zb).start()
+                    o0[z + a] = half[:yl].astype(jnp.bfloat16)
+                    o1[z + a] = half[yl:].astype(jnp.bfloat16)
 
     for k in range(chunks):
         each(k, result)
@@ -395,9 +388,19 @@
         return carry
 
     lax.fori_loop(0, chunks, finish, 0)
-    for zb in range(blocks):
-        store(0, zb).wait()
-        store(1, zb).wait()
+
+def store_kernel(a, b, o0, o1, sem):
+    copies = []
+    parts = sem.shape[1]
+    for f, (src, dst) in enumerate(((a, o0), (b, o1))):
+        size = src.shape[0] // parts
+        for i in range(parts):
+            at = pl.ds(i * size, size)
+            copies.append(pltpu.make_async_copy(src.at[at], dst.at[at], sem.at[f, i]))
+    for c in copies:
+        c.start()
+    for c in copies:
+        c.wait()
 
 
 def tables(cols, chunks, mc, depth, width):
@@ -443,7 +446,7 @@
     bf = jnp.bfloat16
     dma = pltpu.SemaphoreType.DMA
     blocks = zl // 16
-    sems = [dma((2, blocks)), dma((4,)), dma((2, blocks))]
+    sems = [dma((2, blocks)), dma((4,))]
     for n, steps in ((cols, chunks * blocks), (rows, chunks), (rows, chunks), (cols, chunks * blocks)):
         sems += [dma((steps, n)), dma((steps, n)), dma((steps,))]
     field = jax.ShapeDtypeStruct((zl, yl, width), bf)
@@ -469,17 +472,26 @@
         ((chunks, cols, 2, mc, zl, lanes), bf),
         ((zl, lanes, width), jnp.float32),
     ]
+    held = pltpu.VMEM(field.shape, bf)
+    whole = pl.pallas_call(
+        functools.partial(transform_kernel, dims),
+        out_shape=[held, held],
+        in_specs=[anywhere] * 6 + [inside] * 3,
+        out_specs=[inside] * 2,
+        scratch_shapes=[pltpu.VMEM(*v) for v in vmem] + sems,
+        compiler_params=pltpu.CompilerParams(
+            collective_id=0, has_side_effects=True, vmem_limit_bytes=56 << 20
+        ),
+    )(pressure_rhs, scalar_source, tab, gf, gi, back, forward_y, back_y, rates)
     return tuple(
         pl.pallas_call(
-            functools.partial(transform_kernel, dims),
+            store_kernel,
             out_shape=[field, field],
-            in_specs=[anywhere] * 6 + [inside] * 3,
+            in_specs=[inside] * 2,
             out_specs=[anywhere] * 2,
-            scratch_shapes=[pltpu.VMEM(*v) for v in vmem] + sems,
-            compiler_params=pltpu.CompilerParams(
-                collective_id=0, has_side_effects=True, vmem_limit_bytes=67043328
-            ),
-        )(pressure_rhs, scalar_source, tab, gf, gi, back, forward_y, back_y, rates)
+            scratch_shapes=[dma((2, blocks))],
+            compiler_params=pltpu.CompilerParams(vmem_limit_bytes=1 << 20),
+        )(*whole)
     )
 
 

time: 223 us -> 219 us (0.982)
  local copies, waits for them, and re-layouts: 4.87 us -> 0 us
    unnamed x4 -> x0, local copies, waits for them, and re-layouts: 4.87 us -> none
    pallas_call x1 -> x2, Pallas kernels: 217 us -> 218 us  [the longest x1 216 us: fused(): pl.pallas_call(functools.partial(transform_kernel, dims), out_shape=[held...]
where the time goes in v3:
time: 219 us
  Pallas kernels  218 us (100%)
    pallas_call x1, Pallas kernels, fused(): pl.pallas_call(functools.partial(transform_kernel, dims), out_shape=[held...  216 us

profile of v3, /device:TPU:0, one launch (start us, length us, event | category | flops | bytes accessed | tf_op | source)
XLA Modules:
  0.0 218.8 jit_solution(2185787302956996879)
XLA Ops:
  0.6 216.0 %shard_map.104 = (bf16[48,64,384]{2,1,0:T(8,128)(2,1)S(1)}, bf16[48,64,384]{2,1,0:T(8,128)(2,1)S(1)}) custom-call(bf16[48,64,384]{2,1,0:T(8,128)(2,1)} %p_hbm.1, bf16[48,64,384]{2,1,0:T(8,128)(2,1)} %s_hbm.1, bf16[3,128,384]{2,1,0:T(8,128)(2,1)} %constant.8.clone.tab_hbm, bf16[512,768]{1,0:T(8,128)(2,1)} %constant.9.clone.gf_hbm, ...), custom_call_target="tpu_custom_call" | custom-call | tf_op jit(solution)/shard_map/pallas_call | solution.py:476
  216.6 2.2 %shard_map.105 = (bf16[48,64,384]{2,1,0:T(8,128)(2,1)}, bf16[48,64,384]{2,1,0:T(8,128)(2,1)}) custom-call(bf16[48,64,384]{2,1,0:T(8,128)(2,1)S(1)} %get-tuple-element.4.a, bf16[48,64,384]{2,1,0:T(8,128)(2,1)S(1)} %get-tuple-element.5.b), custom_call_target="tpu_custom_call" | custom-call | tf_op jit(solution)/shard_map/pallas_call | solution.py:487
